TPU v7x, 32 devices: a whole 2x2x4 slice. The times are simulated.
32 devices in a mesh: lat: 4 (over x, core), lon: 4 (over z), lev: 2 (over y).
Axes of the slice: x: 2, y: 2, z: 4, core: 2. Of those that a mesh axis runs over, the one named last changes fastest.
Arguments:
- initial_heat: float32 [128, 512, 8, 128], P('lat', 'lon', 'lev'), may hold values from 0.5 to 2
- diffusivity_ratio: float32 [128, 512, 8, 128], P('lat', 'lon', 'lev'), may hold values from 0.03 to 0.15
- forcing_term: float32 [128, 512, 8, 128], P('lat', 'lon', 'lev'), may hold values from -0.2 to 0.2
Outputs:
- standard_deviation_score: float32 [128, 512, 8, 128], P('lat', 'lon', 'lev')
- temperature_end: float32 [128, 512, 8, 128], P('lat', 'lon', 'lev')
All inputs are finite; a program needn't handle non-finite values.
Results may differ from a plain program's by a relative error of at most 0.00002.
Values sent between devices are 32-bit elements; how exact they have to be, the bound alone decides.
A program may use at most 128 MiB of HBM per device.

v0:
```python
import jax
import jax.numpy as jnp
from jax import lax
from jax.sharding import PartitionSpec as P

STEPS = 4


def padded(block, sides, width):
    for axis, dim in sides:
        count = lax.axis_size(axis)
        forward = [(i, i + 1) for i in range(count - 1)]
        forward.append((count - 1, 0))
        backward = [(target, source) for source, target in forward]
        low = lax.ppermute(
            lax.slice_in_dim(block, block.shape[dim] - width, None, axis=dim), axis, forward
        )
        high = lax.ppermute(lax.slice_in_dim(block, 0, width, axis=dim), axis, backward)
        block = jnp.concatenate([low, block, high], axis=dim)
    return block


def without_rim(values, dims):
    for dim in dims:
        values = lax.slice_in_dim(values, 1, values.shape[dim] - 1, axis=dim)
    return values


def shifted_cells(values, dim, start, dims):
    others = [other for other in dims if other != dim]
    values = without_rim(values, others)
    return lax.slice_in_dim(values, start, start + values.shape[dim] - 2, axis=dim)


def march_forward(extended_grid_state, diffusivity_ratio, forcing_term):
    middle = without_rim(extended_grid_state, (0, 1, 2))
    lower = [shifted_cells(extended_grid_state, dim, 0, (0, 1, 2)) for dim in (0, 1, 2)]
    upper = [shifted_cells(extended_grid_state, dim, 2, (0, 1, 2)) for dim in (0, 1, 2)]
    spread = lower[0] + upper[0] + lower[1] + upper[1] + lower[2] + upper[2] - 6.0 * middle
    return middle + diffusivity_ratio * spread + forcing_term


def local(initial_heat, diffusivity_ratio, forcing_term):
    for step in range(STEPS):
        extended_grid_state = padded(initial_heat, (("lat", 0), ("lon", 1), ("lev", 2)), 1)
        initial_heat = march_forward(extended_grid_state, diffusivity_ratio, forcing_term)
    number_of_entries = initial_heat.shape[1] * lax.axis_size("lon")
    guess = 1.0
    moved = initial_heat - guess
    totals, squares = lax.psum(
        (jnp.sum(moved, axis=1, keepdims=True), jnp.sum(moved * moved, axis=1, keepdims=True)),
        "lon",
    )
    row_mean_estimate = guess + totals / number_of_entries
    deviations_from_mean = initial_heat - row_mean_estimate
    line_variance = squares / number_of_entries - totals / number_of_entries * (
        totals / number_of_entries
    )
    standard_deviation_score = deviations_from_mean * lax.rsqrt(line_variance + 0.0001)
    return (standard_deviation_score, initial_heat)


def solution(mesh):
    placed = (
        P("lat", "lon", "lev", None),
        P("lat", "lon", "lev", None),
        P("lat", "lon", "lev", None),
    )
    return jax.shard_map(
        local,
        mesh=mesh,
        in_specs=placed,
        out_specs=(P("lat", "lon", "lev", None), P("lat", "lon", "lev", None)),
        check_vma=False,
    )
```

profile of v0, /device:TPU:0, one launch (start us, length us, event | category | flops | bytes accessed | tf_op | source)
XLA Modules:
  0.0 694.1 jit_solution(3589282031231958471)
XLA Ops:
  7.2 4.8 copy.12
  12.6 2.0 collective-permute-start.1
  15.4 3.4 collective-permute-done
  21.4 2.2 collective-permute-start.2
  23.5 2.1 collective-permute-start.3
  25.6 3.0 collective-permute-done.2
  32.2 52.3 %collective-permute-done.4 = f32[34,130,1,128]{3,1,2,0:T(8,128)S(1)} collective-permute-done((f32[34,130,1,128]{3,1,2,0:T(8,128)S(1)}, f32[34,130,1,128]{3,1,2,0:T(8,128)S(1)}, u32[]{:S(2)}, u32[]{:S(2)}) %collective-permute-start.4) | collective-permute-done | bytes 2263072 | tf_op jit(solution)/shard_map/ppermute | solution.py:15
  84.4 49.2 %collective-permute-done.5 = f32[34,130,1,128]{3,1,2,0:T(8,128)} collective-permute-done((f32[34,130,1,128]{3,1,2,0:T(8,128)S(1)}, f32[34,130,1,128]{3,1,2,0:T(8,128)}, u32[]{:S(2)}, u32[]{:S(2)}) %collective-permute-start.5) | collective-permute-done | bytes 2263072 | tf_op jit(solution)/shard_map/ppermute | solution.py:18
  133.6 30.6 %fusion.31 = f32[32,128,4,128]{3,1,2,0:T(8,128)S(1)} fusion(f32[32,128,4,128]{3,1,2,0:T(8,128)} %copy-done.4, f32[34,130,1,128]{3,1,2,0:T(8,128)} %collective-permute-done.5, f32[34,1,4,128]{3,1,2,0:T(1,128)S(1)} %collective-permute-done.3, f32[34,128,4,128]{3,1,2,0:T(8,128)} %copy-done.3, f32[34,1,4,128]{3,1,2,0:T(1,128)S(1)} %collective-permute-done.2, ...), kind=kLoop, calls=%fused_computation.86 | loop fusion | flops 41943040 | bytes 47656960 | tf_op jit(solution)/shard_map/add | solution.py:40
  166.0 6.2 collective-permute-done.6
  172.4 2.6 collective-permute-start.8
  176.4 2.4 collective-permute-done.8
  183.1 52.3 %collective-permute-done.10 = f32[34,130,1,128]{3,1,2,0:T(8,128)S(1)} collective-permute-done((f32[34,130,1,128]{3,1,2,0:T(8,128)S(1)}, f32[34,130,1,128]{3,1,2,0:T(8,128)S(1)}, u32[]{:S(2)}, u32[]{:S(2)}) %collective-permute-start.10) | collective-permute-done | bytes 2263072 | tf_op jit(solution)/shard_map/ppermute | solution.py:15
  236.8 48.5 %collective-permute-done.11 = f32[34,130,1,128]{3,1,2,0:T(8,128)} collective-permute-done((f32[34,130,1,128]{3,1,2,0:T(8,128)S(1)}, f32[34,130,1,128]{3,1,2,0:T(8,128)}, u32[]{:S(2)}, u32[]{:S(2)}) %collective-permute-start.11) | collective-permute-done | bytes 2263072 | tf_op jit(solution)/shard_map/ppermute | solution.py:18
  285.2 32.6 %fusion.22 = f32[32,128,4,128]{3,1,2,0:T(8,128)S(1)} fusion(f32[32,128,4,128]{3,1,2,0:T(8,128)} %copy-done.2, f32[34,130,1,128]{3,1,2,0:T(8,128)} %collective-permute-done.11, f32[34,1,4,128]{3,1,2,0:T(1,128)S(1)} %collective-permute-done.9, f32[34,1,4,128]{3,1,2,0:T(1,128)S(1)} %collective-permute-done.8, f32[1,128,4,128]{3,1,2,0:T(8,128)S(1)} %collective-permute-done.7, ...), kind=kLoop, calls=%fused_computation.59 | loop fusion | flops 58720256 | bytes 38744064 | tf_op jit(solution)/shard_map/add | solution.py:40
  319.7 6.6 collective-permute-done.12
  326.5 3.8 collective-permute-start.15
  330.3 2.7 collective-permute-done.14
  335.8 52.3 %collective-permute-done.16 = f32[34,130,1,128]{3,1,2,0:T(8,128)S(1)} collective-permute-done((f32[34,130,1,128]{3,1,2,0:T(8,128)S(1)}, f32[34,130,1,128]{3,1,2,0:T(8,128)S(1)}, u32[]{:S(2)}, u32[]{:S(2)}) %collective-permute-start.16) | collective-permute-done | bytes 2263072 | tf_op jit(solution)/shard_map/ppermute | solution.py:15
  389.5 46.9 %collective-permute-done.17 = f32[34,130,1,128]{3,1,2,0:T(8,128)} collective-permute-done((f32[34,130,1,128]{3,1,2,0:T(8,128)S(1)}, f32[34,130,1,128]{3,1,2,0:T(8,128)}, u32[]{:S(2)}, u32[]{:S(2)}) %collective-permute-start.17) | collective-permute-done | bytes 2263072 | tf_op jit(solution)/shard_map/ppermute | solution.py:18
  436.4 32.6 %fusion.13 = f32[32,128,4,128]{3,1,2,0:T(8,128)S(1)} fusion(f32[32,128,4,128]{3,1,2,0:T(8,128)} %copy-done.1, f32[34,130,1,128]{3,1,2,0:T(8,128)} %collective-permute-done.17, f32[34,1,4,128]{3,1,2,0:T(1,128)S(1)} %collective-permute-done.15, f32[34,1,4,128]{3,1,2,0:T(1,128)S(1)} %collective-permute-done.14, ...), kind=kLoop, calls=%fused_computation.32 | loop fusion | flops 58720256 | bytes 38744064 | tf_op jit(solution)/shard_map/add | solution.py:40
  470.9 5.2 collective-permute-done.18
  477.6 4.0 collective-permute-start.21
  481.6 2.3 collective-permute-done.20
  484.6 1.8 collective-permute-start.22
  486.7 52.3 %collective-permute-done.22 = f32[34,130,1,128]{3,1,2,0:T(8,128)S(1)} collective-permute-done((f32[34,130,1,128]{3,1,2,0:T(8,128)S(1)}, f32[34,130,1,128]{3,1,2,0:T(8,128)S(1)}, u32[]{:S(2)}, u32[]{:S(2)}) %collective-permute-start.22) | collective-permute-done | bytes 2263072 | tf_op jit(solution)/shard_map/ppermute | solution.py:15
  538.9 49.4 %collective-permute-done.23 = f32[34,130,1,128]{3,1,2,0:T(8,128)S(1)} collective-permute-done((f32[34,130,1,128]{3,1,2,0:T(8,128)S(1)}, f32[34,130,1,128]{3,1,2,0:T(8,128)S(1)}, u32[]{:S(2)}, u32[]{:S(2)}) %collective-permute-start.23) | collective-permute-done | bytes 2263072 | tf_op jit(solution)/shard_map/ppermute | solution.py:18
  588.3 39.0 %add_reduce_fusion = (f32[32,4,128]{2,1,0:T(4,128)}, f32[32,4,128]{2,1,0:T(4,128)}, f32[32,128,4,128]{3,1,2,0:T(8,128)}) fusion(f32[32,128,4,128]{3,2,1,0:T(4,128)} %param.5, f32[32,128,4,128]{3,1,2,0:T(8,128)} %copy-done, f32[34,130,1,128]{3,1,2,0:T(8,128)S(1)} %collective-permute-done.23, f32[34,1,4,128]{3,1,2,0:T(1,128)S(1)} %collective-permute-done.21, ...), kind=kLoop, calls=%fused_computation.102 | loop fusion | flops 67076096 | bytes 38875136 | tf_op jit(solution)/shard_map/reduce_sum | solution.py:51
  627.3 14.0 %copy.21 = f32[32,128,4,128]{3,2,1,0:T(4,128)} copy(f32[32,128,4,128]{3,1,2,0:T(8,128)} %get-tuple-element.8) | data formatting | bytes 16777216
  641.2 21.7 %all-reduce.3.cloned.1.call-done = (f32[32,1,4,128]{3,2,0,1:T(4,128)}, f32[32,1,4,128]{3,2,0,1:T(4,128)}) async-done(((f32[32,1,4,128]{3,2,0,1:T(4,128)}, f32[32,1,4,128]{3,2,0,1:T(4,128)}), (f32[32,1,4,128]{3,2,0,1:T(4,128)}, f32[32,1,4,128]{3,2,0,1:T(4,128)})) %all-reduce.3.cloned.1.call-update) | async-done | bytes 131088 | tf_op jit(solution)/shard_map/psum | solution.py:50
  663.9 8.7 %subtract_multiply_fusion = f32[32,128,4,128]{3,1,2,0:T(8,128)} fusion(f32[32,128,4,128]{3,1,2,0:T(8,128)} %get-tuple-element.8, f32[32,4,128]{2,1,0:T(4,128)S(1)} %get-tuple-element.34, f32[32,4,128]{2,1,0:T(4,128)S(1)} %get-tuple-element.33), kind=kLoop, calls=%fused_computation.101 | loop fusion | flops 4194304 | bytes 16908288 | tf_op jit(solution)/shard_map/mul | solution.py:59
  672.6 14.2 %copy.20 = f32[32,128,4,128]{3,2,1,0:T(4,128)} copy(f32[32,128,4,128]{3,1,2,0:T(8,128)} %subtract_multiply_fusion) | data formatting | bytes 16777216
  (59 shorter events, 28.0 us)
Async XLA Ops:
  7.2 655.8 %all-reduce.3.cloned.1.call-start = ((), (), s32[]{:S(2)}) async-start(), calls=%async_computation | async-start | bytes 262144 | tf_op jit(solution)/shard_map/psum | solution.py:50
  7.2 11.6 %copy-start.5 = (f32[32,128,4,128]{3,2,1,0:T(4,128)S(1)}, f32[32,128,4,128]{3,2,1,0:T(4,128)}, u32[]{:S(2)}) copy-start(f32[32,128,4,128]{3,2,1,0:T(4,128)} %param.3) | copy-start | bytes 25165828
  12.0 3.4 copy-start.4
  12.1 6.7 collective-permute-start
  12.6 8.6 %collective-permute-start.1 = (f32[1,128,4,128]{3,1,2,0:T(8,128)S(1)}, f32[1,128,4,128]{3,1,2,0:T(8,128)S(1)}, u32[]{:S(2)}, u32[]{:S(2)}) collective-permute-start(f32[1,128,4,128]{3,1,2,0:T(8,128)S(1)} %get-tuple-element.31), channel_id=1, source_target_pairs={{8,0},{16,8},{24,16},{0,24},{9,1},{17,9},{25,17},{1,25},{10,2},{18... | collective-permute-start | bytes 786440 | tf_op jit(solution)/shard_map/ppermute | solution.py:18
  21.2 63.2 %copy-start.3 = (f32[34,128,4,128]{3,1,2,0:T(8,128)}, f32[34,128,4,128]{3,1,2,0:T(8,128)S(1)}, u32[]{:S(2)}) copy-start(f32[34,128,4,128]{3,1,2,0:T(8,128)S(1)} %constant_dynamic-update-slice_fusion) | copy-start | bytes 26738692
  21.4 7.2 %collective-permute-start.2 = (f32[34,1,4,128]{3,1,2,0:T(1,128)S(1)}, f32[34,1,4,128]{3,1,2,0:T(1,128)S(1)}, u32[]{:S(2)}, u32[]{:S(2)}) collective-permute-start(f32[34,1,4,128]{3,1,2,0:T(1,128)S(1)} %get-tuple-element.23), channel_id=1, source_target_pairs={{0,2},{2,4},{4,6},{6,0},{1,3},{3,5},{5,7},{7,1},{8,10},{10,12},{12... | collective-permute-start | bytes 208904 | tf_op jit(solution)/shard_map/ppermute | solution.py:15
  23.5 5.8 collective-permute-start.3
  30.1 54.4 %collective-permute-start.4 = (f32[34,130,1,128]{3,1,2,0:T(8,128)S(1)}, f32[34,130,1,128]{3,1,2,0:T(8,128)S(1)}, u32[]{:S(2)}, u32[]{:S(2)}) collective-permute-start(f32[34,130,1,128]{3,1,2,0:T(8,128)S(1)} %get-tuple-element.15), channel_id=1, source_target_pairs={{0,1},{1,0},{2,3},{3,2},{4,5},{5,4},{6,7},{7,6},{8,9},{9,8},{10,11... | collective-permute-start | bytes 6789128 | tf_op jit(solution)/shard_map/ppermute | solution.py:15
  31.4 102.2 %collective-permute-start.5 = (f32[34,130,1,128]{3,1,2,0:T(8,128)S(1)}, f32[34,130,1,128]{3,1,2,0:T(8,128)}, u32[]{:S(2)}, u32[]{:S(2)}) collective-permute-start(f32[34,130,1,128]{3,1,2,0:T(8,128)S(1)} %get-tuple-element.16), channel_id=1, source_target_pairs={{1,0},{0,1},{3,2},{2,3},{5,4},{4,5},{7,6},{6,7},{9,8},{8,9},{11,10... | collective-permute-start | bytes 6789128 | tf_op jit(solution)/shard_map/ppermute | solution.py:18
  164.2 16.8 %copy-start.2 = (f32[32,128,4,128]{3,1,2,0:T(8,128)}, f32[32,128,4,128]{3,1,2,0:T(8,128)S(1)}, u32[]{:S(2)}) copy-start(f32[32,128,4,128]{3,1,2,0:T(8,128)S(1)} %fusion.31) | copy-start | bytes 25165828
  164.2 8.0 %collective-permute-start.6 = (f32[1,128,4,128]{3,1,2,0:T(8,128)S(1)}, f32[1,128,4,128]{3,1,2,0:T(8,128)S(1)}, u32[]{:S(2)}, u32[]{:S(2)}) collective-permute-start(f32[1,128,4,128]{3,1,2,0:T(8,128)S(1)} %get-tuple-element.29), channel_id=1, source_target_pairs={{0,8},{8,16},{16,24},{24,0},{1,9},{9,17},{17,25},{25,1},{2,10},{10... | collective-permute-start | bytes 786440 | tf_op jit(solution)/shard_map/ppermute | solution.py:15
  164.3 8.0 %collective-permute-start.7 = (f32[1,128,4,128]{3,1,2,0:T(8,128)S(1)}, f32[1,128,4,128]{3,1,2,0:T(8,128)S(1)}, u32[]{:S(2)}, u32[]{:S(2)}) collective-permute-start(f32[1,128,4,128]{3,1,2,0:T(8,128)S(1)} %get-tuple-element.30), channel_id=1, source_target_pairs={{8,0},{16,8},{24,16},{0,24},{9,1},{17,9},{25,17},{1,25},{10,2},{18... | collective-permute-start | bytes 786440 | tf_op jit(solution)/shard_map/ppermute | solution.py:18
  172.4 6.5 collective-permute-start.8
  175.0 5.3 collective-permute-start.9
  181.0 54.4 %collective-permute-start.10 = (f32[34,130,1,128]{3,1,2,0:T(8,128)S(1)}, f32[34,130,1,128]{3,1,2,0:T(8,128)S(1)}, u32[]{:S(2)}, u32[]{:S(2)}) collective-permute-start(f32[34,130,1,128]{3,1,2,0:T(8,128)S(1)} %get-tuple-element.13), channel_id=1, source_target_pairs={{0,1},{1,0},{2,3},{3,2},{4,5},{5,4},{6,7},{7,6},{8,9},{9,8},{10,11... | collective-permute-start | bytes 6789128 | tf_op jit(solution)/shard_map/ppermute | solution.py:15
  182.3 103.0 %collective-permute-start.11 = (f32[34,130,1,128]{3,1,2,0:T(8,128)S(1)}, f32[34,130,1,128]{3,1,2,0:T(8,128)}, u32[]{:S(2)}, u32[]{:S(2)}) collective-permute-start(f32[34,130,1,128]{3,1,2,0:T(8,128)S(1)} %get-tuple-element.14), channel_id=1, source_target_pairs={{1,0},{0,1},{3,2},{2,3},{5,4},{4,5},{7,6},{6,7},{9,8},{8,9},{11,10... | collective-permute-start | bytes 6789128 | tf_op jit(solution)/shard_map/ppermute | solution.py:18
  235.3 1.4 copy-start.6
  317.9 15.9 %copy-start.1 = (f32[32,128,4,128]{3,1,2,0:T(8,128)}, f32[32,128,4,128]{3,1,2,0:T(8,128)S(1)}, u32[]{:S(2)}) copy-start(f32[32,128,4,128]{3,1,2,0:T(8,128)S(1)} %fusion.22) | copy-start | bytes 25165828
  317.9 8.4 %collective-permute-start.12 = (f32[1,128,4,128]{3,1,2,0:T(8,128)S(1)}, f32[1,128,4,128]{3,1,2,0:T(8,128)S(1)}, u32[]{:S(2)}, u32[]{:S(2)}) collective-permute-start(f32[1,128,4,128]{3,1,2,0:T(8,128)S(1)} %get-tuple-element.27), channel_id=1, source_target_pairs={{0,8},{8,16},{16,24},{24,0},{1,9},{9,17},{17,25},{25,1},{2,10},{10... | collective-permute-start | bytes 786440 | tf_op jit(solution)/shard_map/ppermute | solution.py:15
  318.0 8.4 %collective-permute-start.13 = (f32[1,128,4,128]{3,1,2,0:T(8,128)S(1)}, f32[1,128,4,128]{3,1,2,0:T(8,128)S(1)}, u32[]{:S(2)}, u32[]{:S(2)}) collective-permute-start(f32[1,128,4,128]{3,1,2,0:T(8,128)S(1)} %get-tuple-element.28), channel_id=1, source_target_pairs={{8,0},{16,8},{24,16},{0,24},{9,1},{17,9},{25,17},{1,25},{10,2},{18... | collective-permute-start | bytes 786440 | tf_op jit(solution)/shard_map/ppermute | solution.py:18
  326.5 6.6 collective-permute-start.14
  326.5 6.5 collective-permute-start.15
  333.7 54.4 %collective-permute-start.16 = (f32[34,130,1,128]{3,1,2,0:T(8,128)S(1)}, f32[34,130,1,128]{3,1,2,0:T(8,128)S(1)}, u32[]{:S(2)}, u32[]{:S(2)}) collective-permute-start(f32[34,130,1,128]{3,1,2,0:T(8,128)S(1)} %get-tuple-element.11), channel_id=1, source_target_pairs={{0,1},{1,0},{2,3},{3,2},{4,5},{5,4},{6,7},{7,6},{8,9},{9,8},{10,11... | collective-permute-start | bytes 6789128 | tf_op jit(solution)/shard_map/ppermute | solution.py:15
  334.9 101.5 %collective-permute-start.17 = (f32[34,130,1,128]{3,1,2,0:T(8,128)S(1)}, f32[34,130,1,128]{3,1,2,0:T(8,128)}, u32[]{:S(2)}, u32[]{:S(2)}) collective-permute-start(f32[34,130,1,128]{3,1,2,0:T(8,128)S(1)} %get-tuple-element.12), channel_id=1, source_target_pairs={{1,0},{0,1},{3,2},{2,3},{5,4},{4,5},{7,6},{6,7},{9,8},{8,9},{11,10... | collective-permute-start | bytes 6789128 | tf_op jit(solution)/shard_map/ppermute | solution.py:18
  469.0 15.5 %copy-start = (f32[32,128,4,128]{3,1,2,0:T(8,128)}, f32[32,128,4,128]{3,1,2,0:T(8,128)S(1)}, u32[]{:S(2)}) copy-start(f32[32,128,4,128]{3,1,2,0:T(8,128)S(1)} %fusion.13) | copy-start | bytes 25165828
  469.1 7.0 %collective-permute-start.18 = (f32[1,128,4,128]{3,1,2,0:T(8,128)S(1)}, f32[1,128,4,128]{3,1,2,0:T(8,128)S(1)}, u32[]{:S(2)}, u32[]{:S(2)}) collective-permute-start(f32[1,128,4,128]{3,1,2,0:T(8,128)S(1)} %get-tuple-element.25), channel_id=1, source_target_pairs={{0,8},{8,16},{16,24},{24,0},{1,9},{9,17},{17,25},{25,1},{2,10},{10... | collective-permute-start | bytes 786440 | tf_op jit(solution)/shard_map/ppermute | solution.py:15
  469.2 7.5 %collective-permute-start.19 = (f32[1,128,4,128]{3,1,2,0:T(8,128)S(1)}, f32[1,128,4,128]{3,1,2,0:T(8,128)S(1)}, u32[]{:S(2)}, u32[]{:S(2)}) collective-permute-start(f32[1,128,4,128]{3,1,2,0:T(8,128)S(1)} %get-tuple-element.26), channel_id=1, source_target_pairs={{8,0},{16,8},{24,16},{0,24},{9,1},{17,9},{25,17},{1,25},{10,2},{18... | collective-permute-start | bytes 786440 | tf_op jit(solution)/shard_map/ppermute | solution.py:18
  476.8 7.1 %collective-permute-start.20 = (f32[34,1,4,128]{3,1,2,0:T(1,128)S(1)}, f32[34,1,4,128]{3,1,2,0:T(1,128)S(1)}, u32[]{:S(2)}, u32[]{:S(2)}) collective-permute-start(f32[34,1,4,128]{3,1,2,0:T(1,128)S(1)} %get-tuple-element.17), channel_id=1, source_target_pairs={{0,2},{2,4},{4,6},{6,0},{1,3},{3,5},{5,7},{7,1},{8,10},{10,12},{12... | collective-permute-start | bytes 208904 | tf_op jit(solution)/shard_map/ppermute | solution.py:15
  477.6 6.3 collective-permute-start.21
  484.6 54.4 %collective-permute-start.22 = (f32[34,130,1,128]{3,1,2,0:T(8,128)S(1)}, f32[34,130,1,128]{3,1,2,0:T(8,128)S(1)}, u32[]{:S(2)}, u32[]{:S(2)}) collective-permute-start(f32[34,130,1,128]{3,1,2,0:T(8,128)S(1)} %get-tuple-element.9), channel_id=1, source_target_pairs={{0,1},{1,0},{2,3},{3,2},{4,5},{5,4},{6,7},{7,6},{8,9},{9,8},{10,11... | collective-permute-start | bytes 6789128 | tf_op jit(solution)/shard_map/ppermute | solution.py:15
  486.4 102.0 %collective-permute-start.23 = (f32[34,130,1,128]{3,1,2,0:T(8,128)S(1)}, f32[34,130,1,128]{3,1,2,0:T(8,128)S(1)}, u32[]{:S(2)}, u32[]{:S(2)}) collective-permute-start(f32[34,130,1,128]{3,1,2,0:T(8,128)S(1)} %get-tuple-element.10), channel_id=1, source_target_pairs={{1,0},{0,1},{3,2},{2,3},{5,4},{4,5},{7,6},{6,7},{9,8},{8,9},{11,10... | collective-permute-start | bytes 6789128 | tf_op jit(solution)/shard_map/ppermute | solution.py:18
  (1 other events, 1.4 us)
Sparse Core Ops, SparseCore 0:
  627.4 35.5 all-reduce.2
where the time goes:
time: 706 us; the launch traced here: 694 us
  waiting for transfers between devices  460 us (65%)
  other arithmetic  148 us (21%)
  local copies, waits for them, and re-layouts  38.2 us (5%)
  starting transfers between devices  33.2 us (5%)
  between operations  14.7 us (2%)
    ppermute x12, waiting for transfers between devices, padded(): lax.ppermute(lax.slice_in_dim(block, block.shape[dim] - width, None, axis...  241 us
    ppermute x12, waiting for transfers between devices, padded(): lax.ppermute(lax.slice_in_dim(block, 0, width, axis=dim), axis, backward)  198 us
    add x3, other arithmetic, march_forward(): return middle + diffusivity_ratio * spread + forcing_term  95.8 us
    reduce_sum x1, other arithmetic, local(): jnp.sum(moved, axis=1, keepdims=True)  39 us
    unnamed x21, local copies, waits for them, and re-layouts  37.9 us
    psum x1, waiting for transfers between devices, local(): lax.psum((jnp.sum(moved, axis=1, keepdims=True), jnp.sum(moved * moved, a...  21.7 us
    ppermute x12, starting transfers between devices, padded(): lax.ppermute(lax.slice_in_dim(block, 0, width, axis=dim), axis, backward)  21.3 us
  transfers between devices with their start and end apart: 25, of which 21 were waited for; matrix products, arithmetic and copies ran while one was open for 2% of the time, Pallas kernels for 0%

commit v1 on v0

v1 whole, which is shorter than its diff:
```python
import functools

import jax
import jax.numpy as jnp
from jax import lax
from jax.experimental import pallas as pl
from jax.experimental.pallas import tpu as pltpu
from jax.sharding import PartitionSpec as P

STEPS = 4
PAD = 8
XBLOCK = 32
MESH = pl.DeviceIdType.MESH


def march_kernel(
    sizes, chunks, rows,
    heat_in, ratio_in, forcing_in, heat_out, moments_out,
    field, raw, ratio, forcing, xsend, xrecv, stats,
    load_heat, load_ratio, load_forcing, store_heat,
    zsend_sem, zrecv_sem, xsend_sem, xrecv_sem, ysend_sem, yrecv_sem, stat_send, stat_recv,
):
    depth, width, height = sizes
    inner = pl.ds(PAD, width)
    places = {axis: lax.axis_index(axis) for axis in ("lat", "lon", "lev")}
    counts = {axis: lax.axis_size(axis) for axis in ("lat", "lon", "lev")}

    def beside(axis, offset):
        return {axis: lax.rem(places[axis] + offset + counts[axis], counts[axis])}

    def rows_of(c):
        return pl.ds(c * rows, rows)

    def load(c):
        return [
            pltpu.make_async_copy(source.at[rows_of(c)], target.at[rows_of(c)], sem.at[c])
            for source, target, sem in (
                (heat_in, raw, load_heat), (ratio_in, ratio, load_ratio), (forcing_in, forcing, load_forcing),
            )
        ]

    def out_copy(c):
        return pltpu.make_async_copy(raw.at[rows_of(c)], heat_out.at[rows_of(c)], store_heat.at[c])

    def zcopy(side, p, c):
        span = pl.ds(1 + c * rows, rows)
        return pltpu.make_async_remote_copy(
            src_ref=field.at[p, (1, height)[side], span, inner],
            dst_ref=field.at[p, (height + 1, 0)[side], span, inner],
            send_sem=zsend_sem.at[side, p, c], recv_sem=zrecv_sem.at[1 - side, p, c],
            device_id=beside("lev", (-1, 1)[side]), device_id_type=MESH,
        )

    def xcopy(side, p, c):
        return pltpu.make_async_remote_copy(
            src_ref=xsend.at[side, p, c], dst_ref=xrecv.at[1 - side, p, c],
            send_sem=xsend_sem.at[side, p, c], recv_sem=xrecv_sem.at[1 - side, p, c],
            device_id=beside("lon", (-1, 1)[side]), device_id_type=MESH,
        )

    def ycopy(side, p):
        return pltpu.make_async_remote_copy(
            src_ref=field.at[p, pl.ds(1, height), (1, depth)[side], inner],
            dst_ref=field.at[p, pl.ds(1, height), (depth + 1, 0)[side], inner],
            send_sem=ysend_sem.at[side, p], recv_sem=yrecv_sem.at[1 - side, p],
            device_id=beside("lat", (-1, 1)[side]), device_id_type=MESH,
        )

    def stat_copy(offset, c):
        return pltpu.make_async_remote_copy(
            src_ref=stats.at[0, c], dst_ref=stats.at[offset, c],
            send_sem=stat_send.at[offset - 1, c], recv_sem=stat_recv.at[offset - 1, c],
            device_id=beside("lon", offset), device_id_type=MESH,
        )

    def send(p, c):
        for side, end in ((0, 0), (1, chunks - 1)):
            @pl.when(c == end)
            def _():
                ycopy(side, p).start()
        for side in (0, 1):
            zcopy(side, p, c).start()
        for side in (0, 1):
            xcopy(side, p, c).start()

    def sent(p, c):
        for side, end in ((0, 0), (1, chunks - 1)):
            @pl.when(c == end)
            def _():
                ycopy(side, p).wait_send()
        for side in (0, 1):
            zcopy(side, p, c).wait_send()
            xcopy(side, p, c).wait_send()

    def arrived(p, c):
        for side, end in ((1, 0), (0, chunks - 1)):
            @pl.when(c == end)
            def _():
                ycopy(side, p).wait_recv()
        for side in (0, 1):
            xcopy(side, p, c).wait_recv()
        for side in (0, 1):
            zcopy(side, p, c).wait_recv()

    def pack(p, c, i):
        for z in range(height):
            for side, x in ((0, PAD), (1, PAD + width - 1)):
                xsend[side, p, c, pl.ds(i * height + z, 1), :] = field[p, z + 1, c * rows + i + 1, pl.ds(x, 1), :]

    def start_loads(c, carry):
        load(c)[0].start()
        return carry

    def start_others(c, carry):
        for copy in load(c)[1:]:
            copy.start()
        return carry

    lax.fori_loop(0, chunks, start_loads, 0)
    lax.fori_loop(0, chunks, start_others, 0)

    barrier = pltpu.get_barrier_semaphore()
    greeted = [beside("lev", -1), beside("lev", 1), beside("lat", -1), beside("lat", 1)]
    greeted += [beside("lon", offset) for offset in range(1, counts["lon"])]
    for device in greeted:
        pl.semaphore_signal(barrier, inc=1, device_id=device, device_id_type=MESH)
    pl.semaphore_wait(barrier, len(greeted))

    def unpack(c, carry):
        load(c)[0].wait()

        def row(i, carry):
            y = c * rows + i
            for z in range(height):
                field[0, z + 1, y + 1, inner, :] = raw[y, pl.ds(z, width, stride=height), :]
            pack(0, c, i)
            return carry

        lax.fori_loop(0, rows, row, 0)
        send(0, c)
        return carry

    lax.fori_loop(0, chunks, unpack, 0)

    def step(s, carry):
        p = lax.rem(s, 2)
        q = 1 - p

        def chunk(c, carry):
            @pl.when(s == 0)
            def _():
                for copy in load(c)[1:]:
                    copy.wait()

            @pl.when(s >= 1)
            def _():
                sent(q, c)

            arrived(p, c)

            def row(i, carry):
                y = c * rows + i
                for z in range(height):
                    for side, x in ((0, PAD - 1), (1, PAD + width)):
                        field[p, z + 1, y + 1, pl.ds(x, 1), :] = xrecv[side, p, c, pl.ds(i * height + z, 1), :]
                for x in range(0, width, XBLOCK):
                    here = pl.ds(PAD + x, XBLOCK)
                    planes = [field[p, z, y + 1, here, :] for z in range(height + 2)]
                    for z in range(height):
                        middle = planes[z + 1]
                        spread = (
                            field[p, z + 1, y, here, :] + field[p, z + 1, y + 2, here, :]
                            + field[p, z + 1, y + 1, pl.ds(PAD + x - 1, XBLOCK), :]
                            + field[p, z + 1, y + 1, pl.ds(PAD + x + 1, XBLOCK), :]
                            + planes[z] + planes[z + 2] - 6.0 * middle
                        )
                        cells = pl.ds(x * height + z, XBLOCK, stride=height)
                        field[q, z + 1, y + 1, here, :] = middle + ratio[y, cells, :] * spread + forcing[y, cells, :]
                pack(q, c, i)
                return carry

            lax.fori_loop(0, rows, row, 0)

            @pl.when(s < STEPS - 1)
            def _():
                send(q, c)

            @pl.when(s == STEPS - 1)
            def _():
                def finish(i, carry):
                    y = c * rows + i
                    for z in range(height):
                        line = field[q, z + 1, y + 1, inner, :]
                        raw[y, pl.ds(z, width, stride=height), :] = line
                        mean = jnp.sum(line, axis=0, keepdims=True) * (1.0 / width)
                        centred = line - mean
                        stats[0, c, 0, pl.ds(i * height + z, 1), :] = mean
                        stats[0, c, 1, pl.ds(i * height + z, 1), :] = jnp.sum(centred * centred, axis=0, keepdims=True)
                    return carry

                lax.fori_loop(0, rows, finish, 0)
                for offset in range(1, counts["lon"]):
                    stat_copy(offset, c).start()
                out_copy(c).start()

            return carry

        lax.fori_loop(0, chunks, chunk, 0)
        return carry

    lax.fori_loop(0, STEPS, step, 0)

    def combine(c, carry):
        for offset in range(1, counts["lon"]):
            stat_copy(offset, c).wait_recv()
        means = [stats[offset, c, 0] for offset in range(counts["lon"])]
        mean = sum(means[1:], means[0]) * (1.0 / counts["lon"])
        squares = sum([stats[offset, c, 1] for offset in range(1, counts["lon"])], stats[0, c, 1])
        apart = sum([(other - mean) * (other - mean) for other in means[1:]], (means[0] - mean) * (means[0] - mean))
        variance = (squares + width * apart) * (1.0 / (width * counts["lon"]))
        scale = lax.rsqrt(variance + 0.0001)
        for i in range(rows):
            for half in range(2):
                for kind, values in ((0, mean), (1, scale)):
                    moments_out[kind, c * rows + i, pl.ds(half * height, height), :] = values[i * height:(i + 1) * height]
        return carry

    lax.fori_loop(0, chunks, combine, 0)

    def drain(c, carry):
        sent((STEPS - 1) % 2, c)
        for offset in range(1, counts["lon"]):
            stat_copy(offset, c).wait_send()
        out_copy(c).wait()
        return carry

    lax.fori_loop(0, chunks, drain, 0)


def score_kernel(heat, moments, score, end):
    for i in range(heat.shape[0]):
        mean, scale = moments[0, i], moments[1, i]
        values = heat[i]
        end[i] = values
        tall = values.reshape(values.shape[0] // mean.shape[0], *mean.shape)
        score[i] = ((tall - mean[None]) * scale[None]).reshape(values.shape)


def local(initial_heat, diffusivity_ratio, forcing_term):
    depth, width, height, members = initial_heat.shape
    rows = 4
    chunks = depth // rows
    lon = lax.axis_size("lon")
    flat = (depth, width * height, members)
    f32 = jnp.float32
    anywhere = pl.BlockSpec(memory_space=pl.ANY)
    dma = pltpu.SemaphoreType.DMA
    heat, moments = pl.pallas_call(
        functools.partial(march_kernel, (depth, width, height), chunks, rows),
        out_shape=(jax.ShapeDtypeStruct(flat, f32), jax.ShapeDtypeStruct((2, depth, 2 * height, members), f32)),
        in_specs=[anywhere] * 3,
        out_specs=(anywhere, pl.BlockSpec(memory_space=pltpu.VMEM)),
        scratch_shapes=[
            pltpu.VMEM((2, height + 2, depth + 2, width + 2 * PAD, members), f32),
            pltpu.VMEM(flat, f32),
            pltpu.VMEM(flat, f32),
            pltpu.VMEM(flat, f32),
            pltpu.VMEM((2, 2, chunks, rows * height, members), f32),
            pltpu.VMEM((2, 2, chunks, rows * height, members), f32),
            pltpu.VMEM((lon, chunks, 2, rows * height, members), f32),
            dma((chunks,)), dma((chunks,)), dma((chunks,)), dma((chunks,)),
            dma((2, 2, chunks)), dma((2, 2, chunks)),
            dma((2, 2, chunks)), dma((2, 2, chunks)),
            dma((2, 2)), dma((2, 2)),
            dma((lon - 1, chunks)), dma((lon - 1, chunks)),
        ],
        compiler_params=pltpu.CompilerParams(
            collective_id=0, has_side_effects=True, vmem_limit_bytes=60 * 1024 * 1024
        ),
        name="march",
    )(*[a.reshape(flat) for a in (initial_heat, diffusivity_ratio, forcing_term)])
    part = 4
    block = pl.BlockSpec((part,) + flat[1:], lambda i: (i, 0, 0))
    score, end = pl.pallas_call(
        score_kernel,
        grid=(depth // part,),
        out_shape=(jax.ShapeDtypeStruct(flat, f32),) * 2,
        in_specs=[block, pl.BlockSpec((2, part, 2 * height, members), lambda i: (0, i, 0, 0))],
        out_specs=(block, block),
        name="score",
    )(heat, moments)
    return score.reshape(initial_heat.shape), end.reshape(initial_heat.shape)


def solution(mesh):
    placed = P("lat", "lon", "lev", None)
    return jax.shard_map(
        local, mesh=mesh, in_specs=(placed,) * 3, out_specs=(placed,) * 2, check_vma=False
    )
```

time: 706 us -> 386 us (0.55); the launches traced: 694 us -> 386 us
  waiting for transfers between devices: 460 us -> 0 us
  Pallas kernels: 0 us -> 385 us
  other arithmetic: 148 us -> 0 us
  local copies, waits for them, and re-layouts: 38.2 us -> 0 us
  starting transfers between devices: 33.2 us -> 0 us
  between operations: 14.7 us -> 0.64 us
    ppermute x24 -> x0, waiting for transfers between devices: 439 us -> none  [the longest x12 241 us: padded(): lax.ppermute(lax.slice_in_dim(block, block.shape[dim] - width, None, axis...]
    pallas_call x0 -> x2, Pallas kernels: none -> 385 us  [the longest x1 375 us: local(): pl.pallas_call(functools.partial(march_kernel, (depth, width, height), ch...]
    add x3 -> x0, other arithmetic: 95.8 us -> none  [march_forward(): return middle + diffusivity_ratio * spread + forcing_term]
    reduce_sum x1 -> x0, other arithmetic: 39 us -> none  [local(): jnp.sum(moved, axis=1, keepdims=True)]
    unnamed x21 -> x0, local copies, waits for them, and re-layouts: 37.9 us -> none
    ppermute x24 -> x0, starting transfers between devices: 33.2 us -> none  [the longest x12 21.3 us: padded(): lax.ppermute(lax.slice_in_dim(block, 0, width, axis=dim), axis, backward)]
    psum x1 -> x0, waiting for transfers between devices: 21.7 us -> none  [local(): lax.psum((jnp.sum(moved, axis=1, keepdims=True), jnp.sum(moved * moved, a...]
    mul x1 -> x0, other arithmetic: 8.71 us -> none  [local(): deviations_from_mean * lax.rsqrt(line_variance + 0.0001)]
  transfers between devices with their start and end apart: 25 -> 0, of which waited for: 21 -> 0; matrix products, arithmetic and copies ran while one was open for 2% -> 0% of each run, Pallas kernels for 0% -> 0%
where the time goes in v1:
time: 386 us
  Pallas kernels  385 us (100%)
    pallas_call x1, Pallas kernels, local(): pl.pallas_call(functools.partial(march_kernel, (depth, width, height), ch...  375 us
    pallas_call x1, Pallas kernels, local(): pl.pallas_call(score_kernel, grid=(depth // part,), out_shape=(jax.ShapeD...  10.3 us

profile of v1, /device:TPU:0, one launch (start us, length us, event | category | flops | bytes accessed | tf_op | source)
XLA Modules:
  0.0 385.6 jit_solution(4770905785435121364)
XLA Ops:
  0.6 374.6 %march.1 = (f32[32,512,128]{2,1,0:T(8,128)}, f32[2,32,8,128]{3,2,1,0:T(8,128)}) custom-call(f32[32,512,128]{2,1,0:T(8,128)} %bitcast.5, f32[32,512,128]{2,1,0:T(8,128)} %bitcast.6, f32[32,512,128]{2,1,0:T(8,128)} %bitcast.7), custom_call_target="tpu_custom_call" | custom-call | tf_op jit(solution)/shard_map/march/pallas_call | solution.py:258
  375.2 10.3 %score.1 = (f32[32,512,128]{2,1,0:T(8,128)}, f32[32,512,128]{2,1,0:T(8,128)}) custom-call(f32[32,512,128]{2,1,0:T(8,128)} %get-tuple-element.6.heat, f32[2,32,8,128]{3,2,1,0:T(8,128)} %get-tuple-element.7.moments), custom_call_target="tpu_custom_call" | custom-call | tf_op jit(solution)/shard_map/score/pallas_call | solution.py:284

commit v2 on v1

--- a/solution.py
+++ b/solution.py
@@ -15,9 +15,9 @@
 
 def march_kernel(
     sizes, chunks, rows,
-    heat_in, ratio_in, forcing_in, heat_out, moments_out,
-    field, raw, ratio, forcing, xsend, xrecv, stats,
-    load_heat, load_ratio, load_forcing, store_heat,
+    heat_in, ratio_in, forcing_in, raw, moments_out,
+    field, ratio, forcing, xsend, xrecv, stats,
+    load_heat, load_ratio, load_forcing,
     zsend_sem, zrecv_sem, xsend_sem, xrecv_sem, ysend_sem, yrecv_sem, stat_send, stat_recv,
 ):
     depth, width, height = sizes
@@ -38,9 +38,6 @@
                 (heat_in, raw, load_heat), (ratio_in, ratio, load_ratio), (forcing_in, forcing, load_forcing),
             )
         ]
-
-    def out_copy(c):
-        return pltpu.make_async_copy(raw.at[rows_of(c)], heat_out.at[rows_of(c)], store_heat.at[c])
 
     def zcopy(side, p, c):
         span = pl.ds(1 + c * rows, rows)
@@ -124,9 +121,8 @@
     greeted += [beside("lon", offset) for offset in range(1, counts["lon"])]
     for device in greeted:
         pl.semaphore_signal(barrier, inc=1, device_id=device, device_id_type=MESH)
-    pl.semaphore_wait(barrier, len(greeted))
-
-    def unpack(c, carry):
+
+    def unpack(c):
         load(c)[0].wait()
 
         def row(i, carry):
@@ -137,10 +133,33 @@
             return carry
 
         lax.fori_loop(0, rows, row, 0)
+
+    def unpack_send(c, carry):
+        unpack(c)
         send(0, c)
         return carry
 
-    lax.fori_loop(0, chunks, unpack, 0)
+    unpack(0)
+    pl.semaphore_wait(barrier, len(greeted))
+    send(0, 0)
+    lax.fori_loop(1, chunks, unpack_send, 0)
+
+    def combine(c):
+        for offset in range(1, counts["lon"]):
+            stat_copy(offset, c).wait_recv()
+        means = [stats[offset, c, 0] for offset in range(counts["lon"])]
+        mean = sum(means[1:], means[0]) * (1.0 / counts["lon"])
+        squares = sum([stats[offset, c, 1] for offset in range(1, counts["lon"])], stats[0, c, 1])
+        apart = sum([(other - mean) * (other - mean) for other in means[1:]], (means[0] - mean) * (means[0] - mean))
+        variance = (squares + width * apart) * (1.0 / (width * counts["lon"]))
+        scale = lax.rsqrt(variance + 0.0001)
+        for i in range(rows):
+            for half in range(2):
+                for kind, values in ((0, mean), (1, scale)):
+                    moments_out[kind, c * rows + i, pl.ds(half * height, height), :] = values[i * height:(i + 1) * height]
+        for offset in range(1, counts["lon"]):
+            stat_copy(offset, c).wait_send()
+        sent((STEPS - 1) % 2, c)
 
     def step(s, carry):
         p = lax.rem(s, 2)
@@ -201,7 +220,10 @@
                 lax.fori_loop(0, rows, finish, 0)
                 for offset in range(1, counts["lon"]):
                     stat_copy(offset, c).start()
-                out_copy(c).start()
+
+                @pl.when(c >= 1)
+                def _():
+                    combine(c - 1)
 
             return carry
 
@@ -210,45 +232,44 @@
 
     lax.fori_loop(0, STEPS, step, 0)
 
-    def combine(c, carry):
-        for offset in range(1, counts["lon"]):
-            stat_copy(offset, c).wait_recv()
-        means = [stats[offset, c, 0] for offset in range(counts["lon"])]
-        mean = sum(means[1:], means[0]) * (1.0 / counts["lon"])
-        squares = sum([stats[offset, c, 1] for offset in range(1, counts["lon"])], stats[0, c, 1])
-        apart = sum([(other - mean) * (other - mean) for other in means[1:]], (means[0] - mean) * (means[0] - mean))
-        variance = (squares + width * apart) * (1.0 / (width * counts["lon"]))
-        scale = lax.rsqrt(variance + 0.0001)
-        for i in range(rows):
-            for half in range(2):
-                for kind, values in ((0, mean), (1, scale)):
-                    moments_out[kind, c * rows + i, pl.ds(half * height, height), :] = values[i * height:(i + 1) * height]
-        return carry
-
-    lax.fori_loop(0, chunks, combine, 0)
+
+    combine(chunks - 1)
+
+
+def score_kernel(chunks, heat, moments, score, end, scaled, score_sem, end_sem):
+    rows = heat.shape[0] // chunks
+    finish = pltpu.make_async_copy(heat, end, end_sem)
+    finish.start()
+
+    def out_copy(c):
+        span = pl.ds(c * rows, rows)
+        return pltpu.make_async_copy(scaled.at[span], score.at[span], score_sem.at[c])
+
+    def chunk(c, carry):
+        def row(i, carry):
+            y = c * rows + i
+            mean, scale = moments[0, y], moments[1, y]
+            values = heat[y]
+            tall = values.reshape(values.shape[0] // mean.shape[0], *mean.shape)
+            scaled[y] = ((tall - mean[None]) * scale[None]).reshape(values.shape)
+            return carry
+
+        lax.fori_loop(0, rows, row, 0)
+        out_copy(c).start()
+        return carry
 
     def drain(c, carry):
-        sent((STEPS - 1) % 2, c)
-        for offset in range(1, counts["lon"]):
-            stat_copy(offset, c).wait_send()
         out_copy(c).wait()
         return carry
 
+    lax.fori_loop(0, chunks, chunk, 0)
     lax.fori_loop(0, chunks, drain, 0)
-
-
-def score_kernel(heat, moments, score, end):
-    for i in range(heat.shape[0]):
-        mean, scale = moments[0, i], moments[1, i]
-        values = heat[i]
-        end[i] = values
-        tall = values.reshape(values.shape[0] // mean.shape[0], *mean.shape)
-        score[i] = ((tall - mean[None]) * scale[None]).reshape(values.shape)
+    finish.wait()
 
 
 def local(initial_heat, diffusivity_ratio, forcing_term):
     depth, width, height, members = initial_heat.shape
-    rows = 4
+    rows = 2
     chunks = depth // rows
     lon = lax.axis_size("lon")
     flat = (depth, width * height, members)
@@ -257,36 +278,35 @@
     dma = pltpu.SemaphoreType.DMA
     heat, moments = pl.pallas_call(
         functools.partial(march_kernel, (depth, width, height), chunks, rows),
-        out_shape=(jax.ShapeDtypeStruct(flat, f32), jax.ShapeDtypeStruct((2, depth, 2 * height, members), f32)),
+        out_shape=(pltpu.VMEM(flat, f32), pltpu.VMEM((2, depth, 2 * height, members), f32)),
         in_specs=[anywhere] * 3,
-        out_specs=(anywhere, pl.BlockSpec(memory_space=pltpu.VMEM)),
+        out_specs=(pl.BlockSpec(memory_space=pltpu.VMEM),) * 2,
         scratch_shapes=[
             pltpu.VMEM((2, height + 2, depth + 2, width + 2 * PAD, members), f32),
-            pltpu.VMEM(flat, f32),
             pltpu.VMEM(flat, f32),
             pltpu.VMEM(flat, f32),
             pltpu.VMEM((2, 2, chunks, rows * height, members), f32),
             pltpu.VMEM((2, 2, chunks, rows * height, members), f32),
             pltpu.VMEM((lon, chunks, 2, rows * height, members), f32),
-            dma((chunks,)), dma((chunks,)), dma((chunks,)), dma((chunks,)),
+            dma((chunks,)), dma((chunks,)), dma((chunks,)),
             dma((2, 2, chunks)), dma((2, 2, chunks)),
             dma((2, 2, chunks)), dma((2, 2, chunks)),
             dma((2, 2)), dma((2, 2)),
             dma((lon - 1, chunks)), dma((lon - 1, chunks)),
         ],
         compiler_params=pltpu.CompilerParams(
-            collective_id=0, has_side_effects=True, vmem_limit_bytes=60 * 1024 * 1024
+            collective_id=0, has_side_effects=True, vmem_limit_bytes=48 * 1024 * 1024
         ),
         name="march",
     )(*[a.reshape(flat) for a in (initial_heat, diffusivity_ratio, forcing_term)])
-    part = 4
-    block = pl.BlockSpec((part,) + flat[1:], lambda i: (i, 0, 0))
+    parts = min(8, depth)
     score, end = pl.pallas_call(
-        score_kernel,
-        grid=(depth // part,),
+        functools.partial(score_kernel, parts),
         out_shape=(jax.ShapeDtypeStruct(flat, f32),) * 2,
-        in_specs=[block, pl.BlockSpec((2, part, 2 * height, members), lambda i: (0, i, 0, 0))],
-        out_specs=(block, block),
+        in_specs=[pl.BlockSpec(memory_space=pltpu.VMEM)] * 2,
+        out_specs=(anywhere,) * 2,
+        scratch_shapes=[pltpu.VMEM(flat, f32), dma((parts,)), dma(())],
+        compiler_params=pltpu.CompilerParams(vmem_limit_bytes=24 * 1024 * 1024),
         name="score",
     )(heat, moments)
     return score.reshape(initial_heat.shape), end.reshape(initial_heat.shape)

time: 386 us -> 382 us (0.990)
  Pallas kernels: 385 us -> 381 us
    pallas_call x1, Pallas kernels: 10.3 us -> 6.02 us  [local(): pl.pallas_call(functools.partial(score_kernel, parts), out_shape=(jax.Sha...]
where the time goes in v2:
time: 382 us; the launch traced here: 381 us
  Pallas kernels  381 us (100%)
    pallas_call x1, Pallas kernels, local(): pl.pallas_call(functools.partial(march_kernel, (depth, width, height), ch...  375 us

profile of v2, /device:TPU:0, one launch (start us, length us, event | category | flops | bytes accessed | tf_op | source)
XLA Modules:
  0.0 381.5 jit_solution(11605753927494670973)
XLA Ops:
  0.6 374.8 %march.1 = (f32[32,512,128]{2,1,0:T(8,128)S(1)}, f32[2,32,8,128]{3,2,1,0:T(8,128)S(1)}) custom-call(f32[32,512,128]{2,1,0:T(8,128)} %bitcast.5, f32[32,512,128]{2,1,0:T(8,128)} %bitcast.6, f32[32,512,128]{2,1,0:T(8,128)} %bitcast.7), custom_call_target="tpu_custom_call" | custom-call | tf_op jit(solution)/shard_map/march/pallas_call | solution.py:279
  375.5 6.0 %score.1 = (f32[32,512,128]{2,1,0:T(8,128)}, f32[32,512,128]{2,1,0:T(8,128)}) custom-call(f32[32,512,128]{2,1,0:T(8,128)S(1)} %get-tuple-element.6.heat, f32[2,32,8,128]{3,2,1,0:T(8,128)S(1)} %get-tuple-element.7.moments), custom_call_target="tpu_custom_call" | custom-call | tf_op jit(solution)/shard_map/score/pallas_call | solution.py:303

commit v3 on v2

--- a/solution.py
+++ b/solution.py
@@ -113,14 +113,12 @@
             copy.start()
         return carry
 
-    lax.fori_loop(0, chunks, start_loads, 0)
-    lax.fori_loop(0, chunks, start_others, 0)
-
     barrier = pltpu.get_barrier_semaphore()
     greeted = [beside("lev", -1), beside("lev", 1), beside("lat", -1), beside("lat", 1)]
     greeted += [beside("lon", offset) for offset in range(1, counts["lon"])]
     for device in greeted:
         pl.semaphore_signal(barrier, inc=1, device_id=device, device_id_type=MESH)
+    lax.fori_loop(0, chunks, start_loads, 0)
 
     def unpack(c):
         load(c)[0].wait()
@@ -142,6 +140,7 @@
     unpack(0)
     pl.semaphore_wait(barrier, len(greeted))
     send(0, 0)
+    lax.fori_loop(0, chunks, start_others, 0)
     lax.fori_loop(1, chunks, unpack_send, 0)
 
     def combine(c):

time: 382 us -> 381 us (level)
  no operation moved by 1% of the time
where the time goes in v3:
time: 381 us
  Pallas kernels  381 us (100%)
    pallas_call x1, Pallas kernels, local(): pl.pallas_call(functools.partial(march_kernel, (depth, width, height), ch...  375 us

profile of v3, /device:TPU:0, one launch (start us, length us, event | category | flops | bytes accessed | tf_op | source)
XLA Modules:
  0.0 381.2 jit_solution(18259378295340425151)
XLA Ops:
  0.6 374.5 %march.1 = (f32[32,512,128]{2,1,0:T(8,128)S(1)}, f32[2,32,8,128]{3,2,1,0:T(8,128)S(1)}) custom-call(f32[32,512,128]{2,1,0:T(8,128)} %bitcast.5, f32[32,512,128]{2,1,0:T(8,128)} %bitcast.6, f32[32,512,128]{2,1,0:T(8,128)} %bitcast.7), custom_call_target="tpu_custom_call" | custom-call | tf_op jit(solution)/shard_map/march/pallas_call | solution.py:278
  375.2 6.0 %score.1 = (f32[32,512,128]{2,1,0:T(8,128)}, f32[32,512,128]{2,1,0:T(8,128)}) custom-call(f32[32,512,128]{2,1,0:T(8,128)S(1)} %get-tuple-element.6.heat, f32[2,32,8,128]{3,2,1,0:T(8,128)S(1)} %get-tuple-element.7.moments), custom_call_target="tpu_custom_call" | custom-call | tf_op jit(solution)/shard_map/score/pallas_call | solution.py:302
